TPU v7x, 32 devices: a whole 2x2x4 slice. The times are simulated.
32 devices in a mesh: pts: 8 (over z, y), grp: 4 (over x, core).
Axes of the slice: x: 2, y: 2, z: 4, core: 2. Of those that a mesh axis runs over, the one named last changes fastest.
Arguments:
- jacobian: bfloat16 [4096, 3, 3, 384], P(('pts', 'grp')), may hold values from -0.15625 to 0.15625
- owner: int32 [4096, 1], P(('pts', 'grp')), may hold values from 0 to 7; in each aligned block of 128 rows (0 to 127, 128 to 255, ...) at most 32 rows name the same one
- damping: float32 [8, 384], P('pts'), may hold values from 0.2 to 2
Outputs:
- reduced_diag: float32 [8, 384, 384], P('pts', None, 'grp')
- reduced_pair: float32 [8, 384, 384], P('pts', None, 'grp')
Inputs may be any that keep to these rules, and one draw needn't show every extreme that they name: `owner`: among the 128 landmarks of one device at most 32 name the same segment, and in every draw some segment is named by exactly 32 landmarks of some device.
All inputs are finite; a program needn't handle non-finite values.
Results may differ from a plain program's by a relative error of at most 0.0003.
Values may be sent and summed in bfloat16 or wider, within the bound.
A program may use at most 64 MiB of HBM per device.

v0:
```python
import functools

import jax
import jax.numpy as jnp
from jax import lax
from jax.experimental import pallas as pl
from jax.experimental.pallas import tpu as pltpu
from jax.sharding import PartitionSpec as P

MESH = pl.DeviceIdType.MESH
LANES = 128
TILE = 8


def mm(left, right, dims, precise):
    return lax.dot_general(
        left,
        right,
        (dims, ((), ())),
        precision=lax.Precision.HIGHEST if precise else None,
        preferred_element_type=jnp.float32,
    )


NN = ((1,), (0,))
NT = ((1,), (1,))
TN = ((0,), (0,))


def sweep_steps(matrix, rounds):
    size = matrix.shape[0]
    lane_row = lax.broadcasted_iota(jnp.int32, (1, size), 1)
    lane = lax.broadcasted_iota(jnp.int32, (size, size), 1)
    top_row = lax.broadcasted_iota(jnp.int32, (TILE, size), 0)

    def body(_, a):
        for t in range(TILE):
            row = a[t : t + 1, :]
            col = a[:, t : t + 1]
            scaled = jnp.where(lane_row == t, -1.0, row) * (1.0 / a[t : t + 1, t : t + 1])
            new = jnp.where(lane == t, 0.0, a) - col * scaled
            top = jnp.where(top_row == t, scaled, new[:TILE])
            a = jnp.concatenate([top, new[TILE:]], 0)
        a = pltpu.roll(a, size - TILE, 1)
        return jnp.concatenate([a[TILE:], a[:TILE]], 0)

    return lax.fori_loop(0, rounds, body, matrix)


def kernel(
    owners, groups, rows_per, width, capacity,
    planes, owner_row, damp, low_out, pair_out, carried,
    send, recv, sblk, s1, s2, gram, r1, r2, bt, highs,
    a_send, a_recv, d_send, d_recv, d2_recv, g_send, g_recv, b_send, b_recv, c_send, c_recv, own_sem,
):
    me = lax.axis_index("pts")
    grp = lax.axis_index("grp")
    near = grp + 1 - 2 * lax.rem(grp, 2)
    far = lax.rem(grp + 2, groups)
    chunk = width // groups
    nb = width // LANES
    pairs = [(i, j) for i in range(nb) for j in range(i, nb)]
    odd = lax.rem(grp, 2)

    barrier = pltpu.get_barrier_semaphore()

    def greet(off, _):
        pl.semaphore_signal(
            barrier, inc=1, device_id=(lax.rem(me + off, owners), grp), device_id_type=MESH
        )
        return 0

    lax.fori_loop(1, owners, greet, 0)
    for other in (near, far):
        pl.semaphore_signal(barrier, inc=1, device_id=(me, other), device_id_type=MESH)

    clusters, spots, _ = planes.shape
    points = owner_row.shape[1]
    earlier = (
        lax.broadcasted_iota(jnp.int32, (points, points), 0)
        < lax.broadcasted_iota(jnp.int32, (points, points), 1)
    )
    spread = jnp.broadcast_to(owner_row[...], (points, points))
    ahead = jnp.where((spread.T == spread) & earlier, 1, 0)
    place = owner_row[...] * rows_per + jnp.sum(ahead, axis=0, keepdims=True)
    place = jnp.concatenate([place + capacity * r for r in range(spots // points)], 1)
    slot = lax.broadcasted_iota(jnp.int32, (owners * rows_per, spots), 0)
    pick = jnp.where(slot == place, 1.0, 0.0).astype(send.dtype)

    def pack(k):
        send[k] = mm(pick, planes[k], NN, False).astype(send.dtype)

    pack(1)
    pl.semaphore_wait(barrier, owners - 1 + 2)

    def rows_at(i):
        return pl.ds(pl.multiple_of(i * rows_per, rows_per), rows_per)

    for k in (1, 0, 2):
        if k != 1:
            pack(k)

        def issue(off, _, k=k):
            to = lax.rem(me + off, owners)
            pltpu.make_async_remote_copy(
                src_ref=send.at[k, rows_at(to)],
                dst_ref=recv.at[k, rows_at(me)],
                send_sem=a_send.at[k],
                recv_sem=a_recv.at[k],
                device_id=(to, grp),
                device_id_type=MESH,
            ).start()
            return 0

        lax.fori_loop(1, owners, issue, 0)
    for k in range(3):
        pltpu.make_async_copy(
            send.at[k, rows_at(me)], recv.at[k, rows_at(me)], own_sem.at[k]
        ).start()
    for k in range(3):
        pltpu.make_async_copy(
            send.at[k, rows_at(me)], recv.at[k, rows_at(me)], own_sem.at[k]
        ).wait()

    def await_rows(k):
        part = recv.at[k, pl.ds(0, (owners - 1) * rows_per)]
        pltpu.make_async_copy(part, part, a_recv.at[k]).wait()

    await_rows(1)
    first_copies = []
    own = len(pairs)
    for i in range(nb):
        strip = mm(
            recv[1, :, i * LANES : (i + 1) * LANES], recv[1, :, i * LANES :], TN, False
        )
        for j in range(i, nb):
            n = pairs.index((i, j))
            sblk[n] = strip[:, (j - i) * LANES : (j - i + 1) * LANES]
            copy = pltpu.make_async_remote_copy(
                src_ref=sblk.at[n], dst_ref=s1.at[n],
                send_sem=d_send.at[n], recv_sem=d_recv.at[n],
                device_id=(me, near), device_id_type=MESH,
            )
            copy.start()
            first_copies.append(copy)
    second_copies = []

    def forward(some):
        for n in some:
            first_copies[n].wait_recv()
            sblk[own + n] = sblk[n] + s1[n]
            copy = pltpu.make_async_remote_copy(
                src_ref=sblk.at[own + n], dst_ref=s2.at[n],
                send_sem=d_send.at[own + n], recv_sem=d2_recv.at[n],
                device_id=(me, far), device_id_type=MESH,
            )
            copy.start()
            second_copies.append(copy)

    forward(range(1))

    eye = (
        lax.broadcasted_iota(jnp.int32, (LANES, LANES), 0)
        == lax.broadcasted_iota(jnp.int32, (LANES, LANES), 1)
    )

    def reduced(n):
        second_copies[n].wait_recv()
        i, j = pairs[n]
        total = sblk[own + n] + s2[n]
        if i == j:
            total = total + jnp.where(eye, damp[:, i * LANES : (i + 1) * LANES], 0.0)
        return total

    where_in = {pair: n for n, pair in enumerate(pairs)}
    blocks = {}
    inverses, factors = [], {}
    rounds = LANES // TILE

    sides = ((0, 1), (2, 1), (0, 0), (2, 2), (2, 0))

    def chunk_rows(c):
        return pl.ds(pl.multiple_of(c * chunk, TILE), chunk)

    def near_copy(m, h):
        return pltpu.make_async_remote_copy(
            src_ref=gram.at[m, chunk_rows(1 - odd + 2 * h)], dst_ref=r1.at[m, h],
            send_sem=g_send.at[m, h], recv_sem=g_recv.at[m, h],
            device_id=(me, near), device_id_type=MESH,
        )

    def far_copy(m, h):
        return pltpu.make_async_remote_copy(
            src_ref=gram.at[m, chunk_rows(odd + 2 * h if m < 2 else far)], dst_ref=r2.at[m, h],
            send_sem=g_send.at[m, 2 + h], recv_sem=g_recv.at[m, 2 + h],
            device_id=(me, far), device_id_type=MESH,
        )

    def spread_near(m, h):
        at = chunk_rows(odd + 2 * h)
        return pltpu.make_async_remote_copy(
            src_ref=bt.at[m, at], dst_ref=bt.at[m, at],
            send_sem=b_send.at[m, h], recv_sem=b_recv.at[m, h],
            device_id=(me, near), device_id_type=MESH,
        )

    def far_parts(m):
        return range(2) if m < 2 else range(1)

    def make_grams(k, some):
        await_rows(k)
        for m in some:
            left, right = sides[m]
            gram[m] = mm(recv[left], recv[right], TN, False)
            for h in range(2):
                near_copy(m, h).start()

    def fold_near(some):
        for m in some:
            for h in range(2):
                near_copy(m, h).wait()
                at = chunk_rows(odd + 2 * h)
                gram[m, at, :] = gram[m, at, :] + r1[m, h]
            for h in far_parts(m):
                far_copy(m, h).start()

    def fold_far(m):
        for h in far_parts(m):
            far_copy(m, h).wait()
            if m < 2:
                at = chunk_rows(odd + 2 * h)
                bt[m, at, :] = gram[m, at, :] + r2[m, h]
                spread_near(m, h).start()
            else:
                at = chunk_rows(grp)
                gram[m, at, :] = gram[m, at, :] + r2[m, h]

    def second_near():
        fold_near((1,))
        fold_far(0)

    quarters = 4
    hooks = {
        (0, 1): functools.partial(forward, range(1, own)),
        (0, quarters): functools.partial(make_grams, 0, (0, 2)),
        (1, 1): functools.partial(fold_near, (0,)),
        (1, 2): functools.partial(fold_near, (2,)),
        (1, quarters): functools.partial(make_grams, 2, (1, 3, 4)),
        (2, 1): second_near,
        (2, 2): functools.partial(fold_near, (3,)),
        (2, 3): functools.partial(fold_near, (4,)),
    }

    def block(i, j):
        if (i, j) not in blocks:
            blocks[i, j] = reduced(where_in[i, j])
        return blocks[i, j]

    for i in range(nb):
        a = block(i, i)
        for part in range(1, quarters + 1):
            a = sweep_steps(a, rounds // quarters)
            if part < quarters and (i, part) in hooks:
                hooks.pop((i, part))()
        a = -a
        inverses.append(a)
        for j in range(i + 1, nb):
            factors[i, j] = mm(a, block(i, j), NN, True)
        if (i, quarters) in hooks:
            hooks.pop((i, quarters))()
        for j in range(i + 1, nb):
            for k in range(j, nb):
                blocks[j, k] = block(j, k) - mm(block(i, j), factors[i, k], TN, True)
    for key in sorted(hooks):
        hooks[key]()
    mine = chunk_rows(grp)

    def eliminate(m):
        for h in range(2):
            spread_near(m, h).wait()
        for j in range(1, nb):
            value = bt[m, :, j * LANES : (j + 1) * LANES]
            for i in range(j):
                value = value - mm(
                    bt[m, :, i * LANES : (i + 1) * LANES], factors[i, j], NN, True
                )
            bt[m, :, j * LANES : (j + 1) * LANES] = value
        return jnp.concatenate(
            [
                mm(bt[m, mine, i * LANES : (i + 1) * LANES], inverses[i], NN, True)
                for i in range(nb)
            ],
            1,
        )

    fold_far(1)
    solved_low = eliminate(0)
    fold_far(2)
    low_out[...] = gram[2, mine, :] - mm(solved_low, bt[0], NT, True)
    solved_high = eliminate(1)
    fold_far(3)
    highs[...] = gram[3, mine, :] - mm(solved_high, bt[1], NT, True)
    carry = pltpu.make_async_remote_copy(
        src_ref=highs, dst_ref=carried, send_sem=c_send, recv_sem=c_recv,
        device_id=(lax.rem(me + 1, owners), grp), device_id_type=MESH,
    )
    carry.start()
    fold_far(4)
    pair_out[...] = gram[4, mine, :] - mm(solved_high, bt[0], NT, True)
    for copy in first_copies + second_copies:
        copy.wait_send()
    for k in range(3):
        part = send.at[k, pl.ds(0, (owners - 1) * rows_per)]
        pltpu.make_async_copy(part, part, a_send.at[k]).wait()
    carry.wait()


def finish(low, pair, carried, diag_out, pair_out):
    diag_out[...] = low[...] + carried[...]
    pair_out[...] = pair[...]


def local(jacobian, owner, damping):
    points, clusters, residuals, width = jacobian.shape
    owners = lax.axis_size("pts")
    groups = lax.axis_size("grp")
    capacity = max(2, 2 * points // owners)
    rows_per = -(-residuals * capacity // 16) * 16
    total = owners * rows_per
    planes = jnp.transpose(jacobian, (1, 2, 0, 3)).reshape(clusters, residuals * points, width)
    chunk = width // groups
    nb = width // LANES
    blocks = nb * (nb + 1) // 2
    vmem = pl.BlockSpec(memory_space=pltpu.VMEM)
    dma = pltpu.SemaphoreType.DMA
    low, pair, carried = pl.pallas_call(
        functools.partial(kernel, owners, groups, rows_per, width, capacity),
        out_shape=[jax.ShapeDtypeStruct((chunk, width), jnp.float32)] * 3,
        in_specs=[vmem] * 3,
        out_specs=[vmem] * 3,
        scratch_shapes=[
            pltpu.VMEM((clusters, total, width), jacobian.dtype),
            pltpu.VMEM((clusters, total, width), jacobian.dtype),
            pltpu.VMEM((2 * blocks, LANES, LANES), jnp.float32),
            pltpu.VMEM((blocks, LANES, LANES), jnp.float32),
            pltpu.VMEM((blocks, LANES, LANES), jnp.float32),
            pltpu.VMEM((5, width, width), jnp.float32),
            pltpu.VMEM((5, 2, chunk, width), jnp.float32),
            pltpu.VMEM((5, 2, chunk, width), jnp.float32),
            pltpu.VMEM((2, width, width), jnp.float32),
            pltpu.VMEM((chunk, width), jnp.float32),
            dma((3,)), dma((3,)),
            dma((2 * blocks,)), dma((blocks,)), dma((blocks,)),
            dma((5, 4)), dma((5, 4)),
            dma((2, 2)), dma((2, 2)),
            dma, dma, dma((3,)),
        ],
        compiler_params=pltpu.CompilerParams(collective_id=0, has_side_effects=True),
    )(planes, owner.reshape(1, points), damping)
    diag, pair = pl.pallas_call(
        finish,
        out_shape=[jax.ShapeDtypeStruct((chunk, width), jnp.float32)] * 2,
        in_specs=[vmem] * 3,
        out_specs=[vmem] * 2,
    )(low, pair, carried)
    return diag.T[None], pair.T[None]


def solution(mesh):
    placed = (P(("pts", "grp"), None, None, None), P(("pts", "grp"), None), P("pts", None))
    return jax.shard_map(
        local,
        mesh=mesh,
        in_specs=placed,
        out_specs=(P("pts", None, "grp"), P("pts", None, "grp")),
        check_vma=False,
    )
```

profile of v0, /device:TPU:0, one launch (start us, length us, event | category | flops | bytes accessed | tf_op | source)
XLA Modules:
  0.0 87.9 jit_solution(2698070060131287933)
XLA Ops:
  0.6 85.5 %shard_map.50 = (f32[96,384]{1,0:T(8,128)}, f32[96,384]{1,0:T(8,128)}, f32[96,384]{1,0:T(8,128)}) custom-call(bf16[3,384,384]{2,1,0:T(8,128)(2,1)} %bitcast.10, s32[1,128]{1,0:T(1,128)} %bitcast.11, f32[1,384]{1,0:T(1,128)} %damp.1), custom_call_target="tpu_custom_call" | custom-call | tf_op jit(solution)/shard_map/pallas_call | solution.py:336
  86.2 1.8 %shard_map.51 = (f32[96,384]{1,0:T(8,128)}, f32[96,384]{1,0:T(8,128)}) custom-call(f32[96,384]{1,0:T(8,128)} %get-tuple-element.7.low, f32[96,384]{1,0:T(8,128)} %get-tuple-element.8.pair, f32[96,384]{1,0:T(8,128)} %get-tuple-element.9.carried), custom_call_target="tpu_custom_call" | custom-call | tf_op jit(solution)/shard_map/pallas_call | solution.py:360
where the time goes:
time: 88.1 us; the launch traced here: 87.9 us
  Pallas kernels  87.3 us (99%)
    pallas_call x1, Pallas kernels, local(): pl.pallas_call(functools.partial(kernel, owners, groups, rows_per, width,...  85.5 us
    pallas_call x1, Pallas kernels, local(): pl.pallas_call(finish, out_shape=[jax.ShapeDtypeStruct((chunk, width), jn...  1.78 us

commit v1 on v0

--- a/solution.py
+++ b/solution.py
@@ -10,6 +10,7 @@
 MESH = pl.DeviceIdType.MESH
 LANES = 128
 TILE = 8
+PANEL = 32
 
 
 def mm(left, right, dims, precise):
@@ -27,30 +28,82 @@
 TN = ((0,), (0,))
 
 
-def sweep_steps(matrix, rounds):
-    size = matrix.shape[0]
-    lane_row = lax.broadcasted_iota(jnp.int32, (1, size), 1)
-    lane = lax.broadcasted_iota(jnp.int32, (size, size), 1)
-    top_row = lax.broadcasted_iota(jnp.int32, (TILE, size), 0)
-
-    def body(_, a):
+def sub_row(tile, r):
+    return jnp.broadcast_to(tile[r : r + 1, :], (TILE, LANES))
+
+
+def sub_lane(tile, c):
+    return jnp.broadcast_to(tile[:, c : c + 1], (TILE, LANES))
+
+
+def invert_panel(tiles, first, group):
+    lane = lax.broadcasted_iota(jnp.int32, (TILE, LANES), 1)
+    sub = lax.broadcasted_iota(jnp.int32, (TILE, LANES), 0)
+    count = len(tiles)
+    for tile in range(count):
+        start = tile * TILE
+        columns = {u: [sub_lane(row[group], first + start + u) for row in tiles] for u in range(TILE)}
         for t in range(TILE):
-            row = a[t : t + 1, :]
-            col = a[:, t : t + 1]
-            scaled = jnp.where(lane_row == t, -1.0, row) * (1.0 / a[t : t + 1, t : t + 1])
-            new = jnp.where(lane == t, 0.0, a) - col * scaled
-            top = jnp.where(top_row == t, scaled, new[:TILE])
-            a = jnp.concatenate([top, new[TILE:]], 0)
-        a = pltpu.roll(a, size - TILE, 1)
-        return jnp.concatenate([a[TILE:], a[:TILE]], 0)
-
-    return lax.fori_loop(0, rounds, body, matrix)
+            at = first + start + t
+            here = sub == t
+            pivot = columns.pop(t)
+            scale = 1.0 / sub_row(pivot[tile], t)
+            for u in columns:
+                lead = sub_row(columns[u][tile], t) * scale
+                columns[u] = [c - p * lead for c, p in zip(columns[u], pivot)]
+                columns[u][tile] = jnp.where(here, lead, columns[u][tile])
+            for part in range(len(tiles[0])):
+                row = sub_row(tiles[tile][part], t) * scale
+                if part == group:
+                    row = jnp.where(lane == at, scale, row)
+                for g in range(count):
+                    old = tiles[g][part]
+                    if part == group:
+                        old = jnp.where(lane == at, 0.0, old)
+                    tiles[g][part] = old - pivot[g] * row
+                tiles[tile][part] = jnp.where(here, row, tiles[tile][part])
+    return tiles
+
+
+def invert(s, between):
+    size = s.shape[0]
+    panels = size // PANEL
+    lane = lax.broadcasted_iota(jnp.int32, (1, size), 1)
+
+    def tiles_of(value):
+        return [
+            [value[g : g + TILE, c : c + LANES] for c in range(0, size, LANES)]
+            for g in range(0, PANEL, TILE)
+        ]
+
+    def updated(j, rows):
+        at = slice(j * PANEL, (j + 1) * PANEL)
+        kept = jnp.where((lane >= j * PANEL) & (lane < (j + 1) * PANEL), 0.0, s[rows, :])
+        return kept - mm(s[rows, at], s[at, :], NN, True)
+
+    def update(j, after):
+        for rows in (slice(0, j * PANEL), slice((j + after) * PANEL, size)):
+            if rows.stop > rows.start:
+                s[rows, :] = updated(j, rows)
+
+    tiles = tiles_of(s[:PANEL, :])
+    for j in range(panels):
+        between(j)
+        if j:
+            update(j - 1, 2)
+        tiles = invert_panel(tiles, j * PANEL % LANES, j * PANEL // LANES)
+        for g in range(PANEL // TILE):
+            for c in range(size // LANES):
+                s[j * PANEL + g * TILE : j * PANEL + (g + 1) * TILE, c * LANES : (c + 1) * LANES] = tiles[g][c]
+        if j + 1 < panels:
+            tiles = tiles_of(updated(j, slice((j + 1) * PANEL, (j + 2) * PANEL)))
+    update(panels - 1, 1)
 
 
 def kernel(
     owners, groups, rows_per, width, capacity,
     planes, owner_row, damp, low_out, pair_out, carried,
-    send, recv, sblk, s1, s2, gram, r1, r2, bt, highs,
+    send, recv, sblk, s1, s2, system, gram, r1, r2, bt, highs,
     a_send, a_recv, d_send, d_recv, d2_recv, g_send, g_recv, b_send, b_recv, c_send, c_recv, own_sem,
 ):
     me = lax.axis_index("pts")
@@ -172,11 +225,6 @@
             total = total + jnp.where(eye, damp[:, i * LANES : (i + 1) * LANES], 0.0)
         return total
 
-    where_in = {pair: n for n, pair in enumerate(pairs)}
-    blocks = {}
-    inverses, factors = [], {}
-    rounds = LANES // TILE
-
     sides = ((0, 1), (2, 1), (0, 0), (2, 2), (2, 0))
 
     def chunk_rows(c):
@@ -239,38 +287,29 @@
         fold_near((1,))
         fold_far(0)
 
-    quarters = 4
+    forward(range(1, own))
+    for n, (i, j) in enumerate(pairs):
+        total = reduced(n)
+        ri, rj = slice(i * LANES, (i + 1) * LANES), slice(j * LANES, (j + 1) * LANES)
+        system[ri, rj] = total
+        if i != j:
+            system[rj, ri] = total.T
+
     hooks = {
-        (0, 1): functools.partial(forward, range(1, own)),
-        (0, quarters): functools.partial(make_grams, 0, (0, 2)),
-        (1, 1): functools.partial(fold_near, (0,)),
-        (1, 2): functools.partial(fold_near, (2,)),
-        (1, quarters): functools.partial(make_grams, 2, (1, 3, 4)),
-        (2, 1): second_near,
-        (2, 2): functools.partial(fold_near, (3,)),
-        (2, 3): functools.partial(fold_near, (4,)),
+        1: functools.partial(make_grams, 0, (0, 2)),
+        2: functools.partial(fold_near, (0,)),
+        3: functools.partial(fold_near, (2,)),
+        8: functools.partial(make_grams, 2, (1, 3, 4)),
+        9: second_near,
+        10: functools.partial(fold_near, (3,)),
+        11: functools.partial(fold_near, (4,)),
     }
 
-    def block(i, j):
-        if (i, j) not in blocks:
-            blocks[i, j] = reduced(where_in[i, j])
-        return blocks[i, j]
-
-    for i in range(nb):
-        a = block(i, i)
-        for part in range(1, quarters + 1):
-            a = sweep_steps(a, rounds // quarters)
-            if part < quarters and (i, part) in hooks:
-                hooks.pop((i, part))()
-        a = -a
-        inverses.append(a)
-        for j in range(i + 1, nb):
-            factors[i, j] = mm(a, block(i, j), NN, True)
-        if (i, quarters) in hooks:
-            hooks.pop((i, quarters))()
-        for j in range(i + 1, nb):
-            for k in range(j, nb):
-                blocks[j, k] = block(j, k) - mm(block(i, j), factors[i, k], TN, True)
+    def between(j):
+        if j in hooks:
+            hooks.pop(j)()
+
+    invert(system, between)
     for key in sorted(hooks):
         hooks[key]()
     mine = chunk_rows(grp)
@@ -278,20 +317,7 @@
     def eliminate(m):
         for h in range(2):
             spread_near(m, h).wait()
-        for j in range(1, nb):
-            value = bt[m, :, j * LANES : (j + 1) * LANES]
-            for i in range(j):
-                value = value - mm(
-                    bt[m, :, i * LANES : (i + 1) * LANES], factors[i, j], NN, True
-                )
-            bt[m, :, j * LANES : (j + 1) * LANES] = value
-        return jnp.concatenate(
-            [
-                mm(bt[m, mine, i * LANES : (i + 1) * LANES], inverses[i], NN, True)
-                for i in range(nb)
-            ],
-            1,
-        )
+        return mm(bt[m, mine, :], system[...], NN, True)
 
     fold_far(1)
     solved_low = eliminate(0)
@@ -344,6 +370,7 @@
             pltpu.VMEM((2 * blocks, LANES, LANES), jnp.float32),
             pltpu.VMEM((blocks, LANES, LANES), jnp.float32),
             pltpu.VMEM((blocks, LANES, LANES), jnp.float32),
+            pltpu.VMEM((width, width), jnp.float32),
             pltpu.VMEM((5, width, width), jnp.float32),
             pltpu.VMEM((5, 2, chunk, width), jnp.float32),
             pltpu.VMEM((5, 2, chunk, width), jnp.float32),

time: 88.1 us -> 77.2 us (0.88)
  Pallas kernels: 87.3 us -> 76.4 us
    pallas_call x1, Pallas kernels: 85.5 us -> 74.6 us  [local(): pl.pallas_call(functools.partial(kernel, owners, groups, rows_per, width,...]
where the time goes in v1:
time: 77.2 us; the launch traced here: 77 us
  Pallas kernels  76.4 us (99%)
    pallas_call x1, Pallas kernels, local(): pl.pallas_call(functools.partial(kernel, owners, groups, rows_per, width,...  74.6 us
    pallas_call x1, Pallas kernels, local(): pl.pallas_call(finish, out_shape=[jax.ShapeDtypeStruct((chunk, width), jn...  1.78 us

profile of v1, /device:TPU:0, one launch (start us, length us, event | category | flops | bytes accessed | tf_op | source)
XLA Modules:
  0.0 77.0 jit_solution(2421468884223024830)
XLA Ops:
  0.6 74.6 %shard_map.50 = (f32[96,384]{1,0:T(8,128)}, f32[96,384]{1,0:T(8,128)}, f32[96,384]{1,0:T(8,128)}) custom-call(bf16[3,384,384]{2,1,0:T(8,128)(2,1)} %bitcast.10, s32[1,128]{1,0:T(1,128)} %bitcast.11, f32[1,384]{1,0:T(1,128)} %damp.1), custom_call_target="tpu_custom_call" | custom-call | tf_op jit(solution)/shard_map/pallas_call | solution.py:362
  75.2 1.8 %shard_map.51 = (f32[96,384]{1,0:T(8,128)}, f32[96,384]{1,0:T(8,128)}) custom-call(f32[96,384]{1,0:T(8,128)} %get-tuple-element.7.low, f32[96,384]{1,0:T(8,128)} %get-tuple-element.8.pair, f32[96,384]{1,0:T(8,128)} %get-tuple-element.9.carried), custom_call_target="tpu_custom_call" | custom-call | tf_op jit(solution)/shard_map/pallas_call | solution.py:387

commit v2 on v1

v2 whole, which is shorter than its diff:
```python
import functools

import jax
import jax.numpy as jnp
from jax import lax
from jax.experimental import pallas as pl
from jax.experimental.pallas import tpu as pltpu
from jax.sharding import PartitionSpec as P

MESH = pl.DeviceIdType.MESH
LANES = 128
TILE = 8
PANEL = 32
BATCHES = 8


def mm(left, right, dims, precise):
    return lax.dot_general(
        left,
        right,
        (dims, ((), ())),
        precision=lax.Precision.HIGHEST if precise else None,
        preferred_element_type=jnp.float32,
    )


NN = ((1,), (0,))
NT = ((1,), (1,))
TN = ((0,), (0,))


def sub_row(tile, r):
    return jnp.broadcast_to(tile[r : r + 1, :], (TILE, LANES))


def sub_lane(tile, c):
    return jnp.broadcast_to(tile[:, c : c + 1], (TILE, LANES))


def invert_panel(tiles, first, group):
    lane = lax.broadcasted_iota(jnp.int32, (TILE, LANES), 1)
    sub = lax.broadcasted_iota(jnp.int32, (TILE, LANES), 0)
    count = len(tiles)
    for tile in range(count):
        start = tile * TILE
        columns = {u: [sub_lane(row[group], first + start + u) for row in tiles] for u in range(TILE)}
        for t in range(TILE):
            at = first + start + t
            here = sub == t
            pivot = columns.pop(t)
            scale = 1.0 / sub_row(pivot[tile], t)
            for u in columns:
                lead = sub_row(columns[u][tile], t) * scale
                columns[u] = [c - p * lead for c, p in zip(columns[u], pivot)]
                columns[u][tile] = jnp.where(here, lead, columns[u][tile])
            for part in range(len(tiles[0])):
                row = sub_row(tiles[tile][part], t) * scale
                if part == group:
                    row = jnp.where(lane == at, scale, row)
                for g in range(count):
                    old = tiles[g][part]
                    if part == group:
                        old = jnp.where(lane == at, 0.0, old)
                    tiles[g][part] = old - pivot[g] * row
                tiles[tile][part] = jnp.where(here, row, tiles[tile][part])
    return tiles


def invert(s, between):
    size = s.shape[0]
    panels = size // PANEL
    lane = lax.broadcasted_iota(jnp.int32, (1, size), 1)

    def tiles_of(value):
        return [
            [value[g : g + TILE, c : c + LANES] for c in range(0, size, LANES)]
            for g in range(0, PANEL, TILE)
        ]

    def updated(j, rows):
        at = slice(j * PANEL, (j + 1) * PANEL)
        kept = jnp.where((lane >= j * PANEL) & (lane < (j + 1) * PANEL), 0.0, s[rows, :])
        return kept - mm(s[rows, at], s[at, :], NN, True)

    def update(j, after):
        for rows in (slice(0, j * PANEL), slice((j + after) * PANEL, size)):
            if rows.stop > rows.start:
                s[rows, :] = updated(j, rows)

    tiles = tiles_of(s[:PANEL, :])
    for j in range(panels):
        between(j)
        if j:
            update(j - 1, 2)
        tiles = invert_panel(tiles, j * PANEL % LANES, j * PANEL // LANES)
        for g in range(PANEL // TILE):
            for c in range(size // LANES):
                s[j * PANEL + g * TILE : j * PANEL + (g + 1) * TILE, c * LANES : (c + 1) * LANES] = tiles[g][c]
        if j + 1 < panels:
            tiles = tiles_of(updated(j, slice((j + 1) * PANEL, (j + 2) * PANEL)))
    update(panels - 1, 1)


def partner(me, r, owners):
    out, bit = 0, 1
    while bit < owners:
        mine, flip = lax.rem(me // bit, 2), (r // bit) % 2
        out = out + bit * (mine + flip - 2 * mine * flip)
        bit *= 2
    return out


def kernel(
    owners, groups, rows_per, width, capacity,
    planes, owner_row, damp, low_out, pair_out, carried,
    send, rows, system, part, other, window, chunks, highs,
    a_send, a_recv, own_sem, f_send, f_recv, n_send, n_recv, w_send, w_recv, c_send, c_recv,
):
    me = lax.axis_index("pts")
    grp = lax.axis_index("grp")
    near = grp + 1 - 2 * lax.rem(grp, 2)
    far = lax.rem(grp + 2, groups)
    chunk = width // groups
    nb = width // LANES
    batches = min(owners, BATCHES)
    units = owners // batches
    unit_rows = units * rows_per

    barrier = pltpu.get_barrier_semaphore()

    def greet(r, _):
        pl.semaphore_signal(
            barrier, inc=1, device_id=(partner(me, r, owners), grp), device_id_type=MESH
        )
        return 0

    lax.fori_loop(1, owners, greet, 0)
    for peer in (near, far):
        pl.semaphore_signal(barrier, inc=1, device_id=(me, peer), device_id_type=MESH)

    clusters, spots, _ = planes.shape
    points = owner_row.shape[1]
    earlier = (
        lax.broadcasted_iota(jnp.int32, (points, points), 0)
        < lax.broadcasted_iota(jnp.int32, (points, points), 1)
    )
    spread = jnp.broadcast_to(owner_row[...], (points, points))
    ahead = jnp.where((spread.T == spread) & earlier, 1, 0)
    place = owner_row[...] * rows_per + jnp.sum(ahead, axis=0, keepdims=True)
    place = jnp.concatenate([place + capacity * r for r in range(spots // points)], 1)
    slot = lax.broadcasted_iota(jnp.int32, (owners * rows_per, spots), 0)
    pick = jnp.where(slot == place, 1.0, 0.0).astype(send.dtype)

    def pack(k):
        send[k] = mm(pick, planes[k], NN, False).astype(send.dtype)

    def rows_at(i):
        return pl.ds(pl.multiple_of(i * rows_per, rows_per), rows_per)

    def landing(b, side):
        return pl.ds((2 * b + side) * unit_rows, unit_rows)

    def own_copy(k):
        return pltpu.make_async_copy(
            send.at[k, rows_at(me)], rows.at[k, pl.ds(0, rows_per)], own_sem.at[k]
        )

    def issue(k, b):
        def one(i, _):
            r = b * units + i
            to = partner(me, r, owners)
            at = 2 * b * unit_rows + i * rows_per
            pltpu.make_async_remote_copy(
                src_ref=send.at[k, rows_at(to)],
                dst_ref=rows.at[k, pl.ds(pl.multiple_of(at, rows_per), rows_per)],
                send_sem=a_send.at[k], recv_sem=a_recv.at[k, b],
                device_id=(to, grp), device_id_type=MESH,
            ).start()
            return 0

        if b == 0:
            own_copy(k).start()
        if units == 1:
            if b:
                one(0, 0)
        else:
            lax.fori_loop(0 if b else 1, units, one, 0)

    far_copies = {}

    def arrive(k, b):
        remote = unit_rows if b else unit_rows - rows_per
        if remote:
            taken = rows.at[k, pl.ds(0, remote)]
            pltpu.make_async_copy(taken, taken, a_recv.at[k, b]).wait()
        if b == 0:
            own_copy(k).wait()
        copy = pltpu.make_async_remote_copy(
            src_ref=rows.at[k, landing(b, 0)], dst_ref=rows.at[k, landing(b, 1)],
            send_sem=f_send.at[k, b], recv_sem=f_recv.at[k, b],
            device_id=(me, far), device_id_type=MESH,
        )
        copy.start()
        far_copies[k, b] = copy

    def landed(k, some):
        for b in some:
            far_copies[k, b].wait_recv()

    def span(some):
        return slice(2 * some[0] * unit_rows, 2 * (some[-1] + 1) * unit_rows)

    half = -(-2 * chunk // LANES) * LANES
    start = pl.multiple_of(grp // 2 * (width - half), LANES)

    def add_full(n, left, right, some):
        value = mm(rows[left, span(some), :], rows[right, span(some), :], TN, False)
        part[n] = value if some[0] == 0 else part[n] + value

    def add_window(m, left, right, some):
        value = mm(
            rows[left, span(some), pl.ds(start, half)], rows[right, span(some), :], TN, False
        )
        window[m] = value if some[0] == 0 else window[m] + value

    def full_copy(n):
        return pltpu.make_async_remote_copy(
            src_ref=part.at[n], dst_ref=other.at[n],
            send_sem=n_send.at[n], recv_sem=n_recv.at[n],
            device_id=(me, near), device_id_type=MESH,
        )

    def in_window(g):
        return pl.ds(pl.multiple_of(g * chunk - start, TILE), chunk)

    def window_copy(m):
        return pltpu.make_async_remote_copy(
            src_ref=window.at[m, in_window(near)], dst_ref=chunks.at[m],
            send_sem=w_send.at[m], recv_sem=w_recv.at[m],
            device_id=(me, near), device_id_type=MESH,
        )

    mine = pl.ds(pl.multiple_of(grp * chunk, TILE), chunk)

    def summed(n):
        full_copy(n).wait()
        other[n] = part[n] + other[n]

    def own_chunk(m):
        window_copy(m).wait()
        return window[m, in_window(grp), :] + chunks[m]

    pack(1)
    pl.semaphore_wait(barrier, owners - 1 + 2)
    everything = list(range(batches))
    early, late = everything[: batches // 2], everything[batches // 2 :]
    for b in everything:
        issue(1, b)
    pack(2)
    for b in early:
        arrive(1, b)
        issue(2, b)
    pack(0)
    arrive(2, 0)
    issue(0, 0)
    for b in late:
        arrive(1, b)
        issue(2, b)
        if b == late[0]:
            landed(1, early)
            add_full(0, 1, 1, early)
        if b - len(early) + 1 in early:
            arrive(2, b - len(early) + 1)
            issue(0, b - len(early) + 1)
    landed(1, late)
    add_full(0, 1, 1, late)
    full_copy(0).start()
    full_copy(0).wait()
    eye = (
        lax.broadcasted_iota(jnp.int32, (LANES, LANES), 0)
        == lax.broadcasted_iota(jnp.int32, (LANES, LANES), 1)
    )
    system[...] = part[0] + other[0]
    for i in range(nb):
        at = slice(i * LANES, (i + 1) * LANES)
        system[at, at] = system[at, at] + jnp.where(eye, damp[:, at], 0.0)

    def grams_high():
        landed(2, everything)
        add_full(1, 2, 1, everything)
        full_copy(1).start()
        add_window(0, 2, 2, everything)
        window_copy(0).start()

    plan = {
        0: [(2, late[0])], 1: [(0, 0)], 2: [(2, late[1])], 3: [(0, 1)], 4: [(2, late[2])],
        5: [(0, 2)], 6: [(2, late[3])], 7: [(0, 3)], 9: [(0, late[0])], 11: [(0, late[1])],
    }

    def between(j):
        for k, b in plan.get(j, ()):
            arrive(k, b)
            if k == 2:
                issue(0, b)
        if j == 10:
            grams_high()

    invert(system, between)
    summed(1)
    solved_high = mm(other[1, mine, :], system[...], NN, True)
    arrive(0, late[2])
    highs[...] = own_chunk(0) - mm(solved_high, other[1], NT, True)
    carry = pltpu.make_async_remote_copy(
        src_ref=highs, dst_ref=carried, send_sem=c_send, recv_sem=c_recv,
        device_id=(lax.rem(me + 1, owners), grp), device_id_type=MESH,
    )
    carry.start()
    arrive(0, late[3])
    first = everything[:-1]
    for some in (first, everything[-1:]):
        landed(0, some)
        add_full(2, 0, 1, some)
        if some is not first:
            full_copy(2).start()
        add_window(1, 0, 0, some)
        add_window(2, 2, 0, some)
    window_copy(1).start()
    window_copy(2).start()
    summed(2)
    solved_low = mm(other[2, mine, :], system[...], NN, True)
    low_out[...] = own_chunk(1) - mm(solved_low, other[2], NT, True)
    pair_out[...] = own_chunk(2) - mm(solved_high, other[2], NT, True)
    for copy in far_copies.values():
        copy.wait_send()
    for k in range(clusters):
        sent = send.at[k, pl.ds(0, (owners - 1) * rows_per)]
        pltpu.make_async_copy(sent, sent, a_send.at[k]).wait()
    carry.wait()


def finish(low, pair, carried, diag_out, pair_out):
    diag_out[...] = low[...] + carried[...]
    pair_out[...] = pair[...]


def local(jacobian, owner, damping):
    points, clusters, residuals, width = jacobian.shape
    owners = lax.axis_size("pts")
    groups = lax.axis_size("grp")
    capacity = max(2, 2 * points // owners)
    rows_per = -(-residuals * capacity // 16) * 16
    total = owners * rows_per
    planes = jnp.transpose(jacobian, (1, 2, 0, 3)).reshape(clusters, residuals * points, width)
    chunk = width // groups
    half = -(-2 * chunk // LANES) * LANES
    batches = min(owners, BATCHES)
    vmem = pl.BlockSpec(memory_space=pltpu.VMEM)
    dma = pltpu.SemaphoreType.DMA
    low, pair, carried = pl.pallas_call(
        functools.partial(kernel, owners, groups, rows_per, width, capacity),
        out_shape=[jax.ShapeDtypeStruct((chunk, width), jnp.float32)] * 3,
        in_specs=[vmem] * 3,
        out_specs=[vmem] * 3,
        scratch_shapes=[
            pltpu.VMEM((clusters, total, width), jacobian.dtype),
            pltpu.VMEM((clusters, 2 * total, width), jacobian.dtype),
            pltpu.VMEM((width, width), jnp.float32),
            pltpu.VMEM((3, width, width), jnp.float32),
            pltpu.VMEM((3, width, width), jnp.float32),
            pltpu.VMEM((3, half, width), jnp.float32),
            pltpu.VMEM((3, chunk, width), jnp.float32),
            pltpu.VMEM((chunk, width), jnp.float32),
            dma((clusters,)), dma((clusters, batches)), dma((clusters,)),
            dma((clusters, batches)), dma((clusters, batches)),
            dma((3,)), dma((3,)), dma((3,)), dma((3,)),
            dma, dma,
        ],
        compiler_params=pltpu.CompilerParams(collective_id=0, has_side_effects=True),
    )(planes, owner.reshape(1, points), damping)
    diag, pair = pl.pallas_call(
        finish,
        out_shape=[jax.ShapeDtypeStruct((chunk, width), jnp.float32)] * 2,
        in_specs=[vmem] * 3,
        out_specs=[vmem] * 2,
    )(low, pair, carried)
    return diag.T[None], pair.T[None]


def solution(mesh):
    placed = (P(("pts", "grp"), None, None, None), P(("pts", "grp"), None), P("pts", None))
    return jax.shard_map(
        local,
        mesh=mesh,
        in_specs=placed,
        out_specs=(P("pts", None, "grp"), P("pts", None, "grp")),
        check_vma=False,
    )
```

time: 77.2 us -> 66.5 us (0.86)
  Pallas kernels: 76.4 us -> 65.7 us
    pallas_call x1, Pallas kernels: 74.6 us -> 64 us  [local(): pl.pallas_call(functools.partial(kernel, owners, groups, rows_per, width,...]
where the time goes in v2:
time: 66.5 us; the launch traced here: 66.4 us
  Pallas kernels  65.7 us (99%)
    pallas_call x1, Pallas kernels, local(): pl.pallas_call(functools.partial(kernel, owners, groups, rows_per, width,...  64 us
    pallas_call x1, Pallas kernels, local(): pl.pallas_call(finish, out_shape=[jax.ShapeDtypeStruct((chunk, width), jn...  1.78 us

profile of v2, /device:TPU:0, one launch (start us, length us, event | category | flops | bytes accessed | tf_op | source)
XLA Modules:
  0.0 66.4 jit_solution(884376175766202548)
XLA Ops:
  0.6 64.0 %shard_map.50 = (f32[96,384]{1,0:T(8,128)}, f32[96,384]{1,0:T(8,128)}, f32[96,384]{1,0:T(8,128)}) custom-call(bf16[3,384,384]{2,1,0:T(8,128)(2,1)} %bitcast.10, s32[1,128]{1,0:T(1,128)} %bitcast.11, f32[1,384]{1,0:T(1,128)} %damp.1), custom_call_target="tpu_custom_call" | custom-call | tf_op jit(solution)/shard_map/pallas_call | solution.py:359
  64.6 1.8 %shard_map.51 = (f32[96,384]{1,0:T(8,128)}, f32[96,384]{1,0:T(8,128)}) custom-call(f32[96,384]{1,0:T(8,128)} %get-tuple-element.7.low, f32[96,384]{1,0:T(8,128)} %get-tuple-element.8.pair, f32[96,384]{1,0:T(8,128)} %get-tuple-element.9.carried), custom_call_target="tpu_custom_call" | custom-call | tf_op jit(solution)/shard_map/pallas_call | solution.py:380

commit v3 on v2

--- a/solution.py
+++ b/solution.py
@@ -262,18 +262,25 @@
         issue(2, b)
     pack(0)
     arrive(2, 0)
-    issue(0, 0)
     for b in late:
         arrive(1, b)
         issue(2, b)
         if b == late[0]:
+            for e in early:
+                issue(0, e)
+        if b == late[1]:
             landed(1, early)
             add_full(0, 1, 1, early)
-        if b - len(early) + 1 in early:
-            arrive(2, b - len(early) + 1)
-            issue(0, b - len(early) + 1)
-    landed(1, late)
-    add_full(0, 1, 1, late)
+    for b in early[1:]:
+        arrive(2, b)
+    landed(1, late[:-1])
+    add_full(0, 1, 1, late[:-1])
+    for b in early:
+        arrive(0, b)
+    for b in late[:2]:
+        issue(0, b)
+    landed(1, late[-1:])
+    add_full(0, 1, 1, late[-1:])
     full_copy(0).start()
     full_copy(0).wait()
     eye = (
@@ -292,15 +299,13 @@
         add_window(0, 2, 2, everything)
         window_copy(0).start()
 
-    plan = {
-        0: [(2, late[0])], 1: [(0, 0)], 2: [(2, late[1])], 3: [(0, 1)], 4: [(2, late[2])],
-        5: [(0, 2)], 6: [(2, late[3])], 7: [(0, 3)], 9: [(0, late[0])], 11: [(0, late[1])],
-    }
+    plan = {2: [(2, late[0])], 4: [(2, late[1])], 5: [(2, late[2])], 7: [(2, late[3])], 9: [(0, late[0])], 11: [(0, late[1])]}
 
     def between(j):
         for k, b in plan.get(j, ()):
             arrive(k, b)
-            if k == 2:
+        if j == 2:
+            for b in late[2:]:
                 issue(0, b)
         if j == 10:
             grams_high()
@@ -328,8 +333,9 @@
     window_copy(2).start()
     summed(2)
     solved_low = mm(other[2, mine, :], system[...], NN, True)
-    low_out[...] = own_chunk(1) - mm(solved_low, other[2], NT, True)
-    pair_out[...] = own_chunk(2) - mm(solved_high, other[2], NT, True)
+    both = mm(jnp.concatenate([solved_low, solved_high], 0), other[2], NT, True)
+    low_out[...] = own_chunk(1) - both[:chunk]
+    pair_out[...] = own_chunk(2) - both[chunk:]
     for copy in far_copies.values():
         copy.wait_send()
     for k in range(clusters):

time: 66.5 us -> 62.5 us (0.940); the launches traced: 66.4 us -> 61.6 us
  Pallas kernels: 65.7 us -> 61 us
    pallas_call x1, Pallas kernels: 64 us -> 59.2 us  [local(): pl.pallas_call(functools.partial(kernel, owners, groups, rows_per, width,...]
where the time goes in v3:
time: 62.5 us; the launch traced here: 61.6 us
  Pallas kernels  61 us (98%)
  between operations  0.64 us (1%)
    pallas_call x1, Pallas kernels, local(): pl.pallas_call(functools.partial(kernel, owners, groups, rows_per, width,...  59.2 us
    pallas_call x1, Pallas kernels, local(): pl.pallas_call(finish, out_shape=[jax.ShapeDtypeStruct((chunk, width), jn...  1.78 us

profile of v3, /device:TPU:0, one launch (start us, length us, event | category | flops | bytes accessed | tf_op | source)
XLA Modules:
  0.0 61.6 jit_solution(16872453650551246747)
XLA Ops:
  0.6 59.2 %shard_map.50 = (f32[96,384]{1,0:T(8,128)}, f32[96,384]{1,0:T(8,128)}, f32[96,384]{1,0:T(8,128)}) custom-call(bf16[3,384,384]{2,1,0:T(8,128)(2,1)} %bitcast.10, s32[1,128]{1,0:T(1,128)} %bitcast.11, f32[1,384]{1,0:T(1,128)} %damp.1), custom_call_target="tpu_custom_call" | custom-call | tf_op jit(solution)/shard_map/pallas_call | solution.py:365
  59.8 1.8 %shard_map.51 = (f32[96,384]{1,0:T(8,128)}, f32[96,384]{1,0:T(8,128)}) custom-call(f32[96,384]{1,0:T(8,128)} %get-tuple-element.7.low, f32[96,384]{1,0:T(8,128)} %get-tuple-element.8.pair, f32[96,384]{1,0:T(8,128)} %get-tuple-element.9.carried), custom_call_target="tpu_custom_call" | custom-call | tf_op jit(solution)/shard_map/pallas_call | solution.py:386

commit v4 on v2

--- a/solution.py
+++ b/solution.py
@@ -12,6 +12,7 @@
 TILE = 8
 PANEL = 32
 BATCHES = 8
+RELAYED = 2
 
 
 def mm(left, right, dims, precise):
@@ -112,9 +113,9 @@
 
 def kernel(
     owners, groups, rows_per, width, capacity,
-    planes, owner_row, damp, low_out, pair_out, carried,
-    send, rows, system, part, other, window, chunks, highs,
-    a_send, a_recv, own_sem, f_send, f_recv, n_send, n_recv, w_send, w_recv, c_send, c_recv,
+    planes_in, owner_in, damp_in, low_out, pair_out, carried,
+    planes, owner_row, damp, send, rows, last, system, part, other, window, chunks, highs,
+    in_sem, a_send, a_recv, own_sem, f_send, f_recv, n_send, n_recv, w_send, w_recv, l_send, l_recv, c_send, c_recv,
 ):
     me = lax.axis_index("pts")
     grp = lax.axis_index("grp")
@@ -126,6 +127,12 @@
     units = owners // batches
     unit_rows = units * rows_per
 
+    fetches = [
+        pltpu.make_async_copy(src, dst, in_sem.at[n])
+        for n, (src, dst) in enumerate(((owner_in, owner_row), (planes_in, planes), (damp_in, damp)))
+    ]
+    for fetch in fetches:
+        fetch.start()
     barrier = pltpu.get_barrier_semaphore()
 
     def greet(r, _):
@@ -144,6 +151,7 @@
         lax.broadcasted_iota(jnp.int32, (points, points), 0)
         < lax.broadcasted_iota(jnp.int32, (points, points), 1)
     )
+    fetches[0].wait()
     spread = jnp.broadcast_to(owner_row[...], (points, points))
     ahead = jnp.where((spread.T == spread) & earlier, 1, 0)
     place = owner_row[...] * rows_per + jnp.sum(ahead, axis=0, keepdims=True)
@@ -202,10 +210,22 @@
         )
         copy.start()
         far_copies[k, b] = copy
+        if b >= batches - RELAYED:
+            relay(k, b, 0).start()
+
+    def relay(k, b, side):
+        at = (2 * (b - batches + RELAYED) + side) * unit_rows
+        return pltpu.make_async_remote_copy(
+            src_ref=rows.at[k, landing(b, side)], dst_ref=last.at[k, pl.ds(at, unit_rows)],
+            send_sem=l_send.at[k, b, side], recv_sem=l_recv.at[k, b, side],
+            device_id=(me, near), device_id_type=MESH,
+        )
 
     def landed(k, some):
         for b in some:
             far_copies[k, b].wait_recv()
+            if b >= batches - RELAYED:
+                relay(k, b, 1).start()
 
     def span(some):
         return slice(2 * some[0] * unit_rows, 2 * (some[-1] + 1) * unit_rows)
@@ -250,86 +270,122 @@
         window_copy(m).wait()
         return window[m, in_window(grp), :] + chunks[m]
 
+    fetches[1].wait()
+    fetches[2].wait()
     pack(1)
     pl.semaphore_wait(barrier, owners - 1 + 2)
     everything = list(range(batches))
     early, late = everything[: batches // 2], everything[batches // 2 :]
     for b in everything:
         issue(1, b)
+    arrive(1, 0)
     pack(2)
-    for b in early:
+    issue(2, 0)
+    for b in early[1:]:
         arrive(1, b)
         issue(2, b)
+    arrive(2, 0)
     pack(0)
-    arrive(2, 0)
-    issue(0, 0)
     for b in late:
         arrive(1, b)
         issue(2, b)
-        if b == late[0]:
+        if b == late[1]:
+            for e in early:
+                issue(0, e)
             landed(1, early)
             add_full(0, 1, 1, early)
-        if b - len(early) + 1 in early:
-            arrive(2, b - len(early) + 1)
-            issue(0, b - len(early) + 1)
-    landed(1, late)
-    add_full(0, 1, 1, late)
+    first, tail = everything[: batches - RELAYED], everything[batches - RELAYED :]
+    ends = span(tail)
+    columns = pl.ds(start, half)
+
+    def relayed(k):
+        for b in tail:
+            for side in range(2):
+                relay(k, b, side).wait()
+
+    rest = [b for b in first if b not in early]
+    landed(1, rest)
+    add_full(0, 1, 1, rest)
     full_copy(0).start()
+    for b in early[1:]:
+        arrive(2, b)
+    landed(1, tail)
+    system[...] = mm(rows[1, ends, :], rows[1, ends, :], TN, False)
     full_copy(0).wait()
+    system[...] = system[...] + (part[0] + other[0])
+    relayed(1)
+    system[...] = system[...] + mm(last[1], last[1], TN, False)
     eye = (
         lax.broadcasted_iota(jnp.int32, (LANES, LANES), 0)
         == lax.broadcasted_iota(jnp.int32, (LANES, LANES), 1)
     )
-    system[...] = part[0] + other[0]
     for i in range(nb):
         at = slice(i * LANES, (i + 1) * LANES)
         system[at, at] = system[at, at] + jnp.where(eye, damp[:, at], 0.0)
 
-    def grams_high():
-        landed(2, everything)
-        add_full(1, 2, 1, everything)
-        full_copy(1).start()
-        add_window(0, 2, 2, everything)
-        window_copy(0).start()
-
     plan = {
-        0: [(2, late[0])], 1: [(0, 0)], 2: [(2, late[1])], 3: [(0, 1)], 4: [(2, late[2])],
-        5: [(0, 2)], 6: [(2, late[3])], 7: [(0, 3)], 9: [(0, late[0])], 11: [(0, late[1])],
+        0: [(0, e) for e in early[:2]], 1: [(0, early[2])], 2: [(0, early[3])],
+        3: [(2, late[0])], 4: [(2, late[1])], 5: [(2, late[2])], 7: [(2, late[3])],
+        9: [(0, late[0])], 11: [(0, late[1])],
     }
+    sends = {0: late[0], 2: late[1], 3: late[2], 4: late[3]}
 
     def between(j):
         for k, b in plan.get(j, ()):
             arrive(k, b)
-            if k == 2:
-                issue(0, b)
-        if j == 10:
-            grams_high()
+        if j in sends:
+            issue(0, sends[j])
+        if j == 9:
+            landed(2, first)
+            add_full(1, 2, 1, first)
+            full_copy(1).start()
+            add_window(0, 2, 2, first)
+            window_copy(0).start()
+        if j == 11:
+            landed(2, tail)
 
     invert(system, between)
+    arrive(0, late[2])
     summed(1)
+    relayed(2)
+    other[1] = other[1] + (
+        mm(rows[2, ends, :], rows[1, ends, :], TN, False) + mm(last[2], last[1], TN, False)
+    )
     solved_high = mm(other[1, mine, :], system[...], NN, True)
-    arrive(0, late[2])
-    highs[...] = own_chunk(0) - mm(solved_high, other[1], NT, True)
+    arrive(0, late[3])
+    chunks[0] = own_chunk(0)
+    window[0] = mm(rows[2, ends, columns], rows[2, ends, :], TN, False) + mm(
+        last[2, :, columns], last[2], TN, False
+    )
+    highs[...] = chunks[0] + window[0, in_window(grp), :] - mm(solved_high, other[1], NT, True)
     carry = pltpu.make_async_remote_copy(
         src_ref=highs, dst_ref=carried, send_sem=c_send, recv_sem=c_recv,
         device_id=(lax.rem(me + 1, owners), grp), device_id_type=MESH,
     )
     carry.start()
-    arrive(0, late[3])
-    first = everything[:-1]
-    for some in (first, everything[-1:]):
-        landed(0, some)
-        add_full(2, 0, 1, some)
-        if some is not first:
-            full_copy(2).start()
-        add_window(1, 0, 0, some)
-        add_window(2, 2, 0, some)
+    landed(0, first)
+    add_full(2, 0, 1, first)
+    full_copy(2).start()
+    add_window(1, 0, 0, first)
     window_copy(1).start()
+    add_window(2, 2, 0, first)
     window_copy(2).start()
+    landed(0, tail[:-1])
     summed(2)
+    for m in (1, 2):
+        chunks[m] = own_chunk(m)
+    landed(0, tail[-1:])
+    other[2] = other[2] + mm(rows[0, ends, :], rows[1, ends, :], TN, False)
+    for m, k in ((1, 0), (2, 2)):
+        window[m] = mm(rows[k, ends, columns], rows[0, ends, :], TN, False)
+    relayed(0)
+    other[2] = other[2] + mm(last[0], last[1], TN, False)
     solved_low = mm(other[2, mine, :], system[...], NN, True)
-    low_out[...] = own_chunk(1) - mm(solved_low, other[2], NT, True)
-    pair_out[...] = own_chunk(2) - mm(solved_high, other[2], NT, True)
+    for m, k in ((1, 0), (2, 2)):
+        window[m] = window[m] + mm(last[k, :, columns], last[0], TN, False)
+    both = mm(jnp.concatenate([solved_low, solved_high], 0), other[2], NT, True)
+    low_out[...] = chunks[1] + window[1, in_window(grp), :] - both[:chunk]
+    pair_out[...] = chunks[2] + window[2, in_window(grp), :] - both[chunk:]
     for copy in far_copies.values():
         copy.wait_send()
     for k in range(clusters):
@@ -359,21 +415,25 @@
     low, pair, carried = pl.pallas_call(
         functools.partial(kernel, owners, groups, rows_per, width, capacity),
         out_shape=[jax.ShapeDtypeStruct((chunk, width), jnp.float32)] * 3,
-        in_specs=[vmem] * 3,
+        in_specs=[pl.BlockSpec(memory_space=pl.ANY)] * 3,
         out_specs=[vmem] * 3,
         scratch_shapes=[
+            pltpu.VMEM(planes.shape, planes.dtype),
+            pltpu.VMEM((1, points), owner.dtype),
+            pltpu.VMEM(damping.shape, damping.dtype),
             pltpu.VMEM((clusters, total, width), jacobian.dtype),
             pltpu.VMEM((clusters, 2 * total, width), jacobian.dtype),
+            pltpu.VMEM((clusters, 2 * RELAYED * total // batches, width), jacobian.dtype),
             pltpu.VMEM((width, width), jnp.float32),
             pltpu.VMEM((3, width, width), jnp.float32),
             pltpu.VMEM((3, width, width), jnp.float32),
             pltpu.VMEM((3, half, width), jnp.float32),
             pltpu.VMEM((3, chunk, width), jnp.float32),
             pltpu.VMEM((chunk, width), jnp.float32),
-            dma((clusters,)), dma((clusters, batches)), dma((clusters,)),
+            dma((3,)), dma((clusters,)), dma((clusters, batches)), dma((clusters,)),
             dma((clusters, batches)), dma((clusters, batches)),
             dma((3,)), dma((3,)), dma((3,)), dma((3,)),
-            dma, dma,
+            dma((clusters, batches, 2)), dma((clusters, batches, 2)), dma, dma,
         ],
         compiler_params=pltpu.CompilerParams(collective_id=0, has_side_effects=True),
     )(planes, owner.reshape(1, points), damping)

time: 66.5 us -> 61.1 us (0.919)
  Pallas kernels: 65.7 us -> 60.3 us
    pallas_call x1, Pallas kernels: 64 us -> 58.5 us  [local(): pl.pallas_call(functools.partial(kernel, owners, groups, rows_per, width,...]
where the time goes in v4:
time: 61.1 us; the launch traced here: 60.9 us
  Pallas kernels  60.3 us (99%)
  between operations  0.64 us (1%)
    pallas_call x1, Pallas kernels, local(): pl.pallas_call(functools.partial(kernel, owners, groups, rows_per, width,...  58.5 us
    pallas_call x1, Pallas kernels, local(): pl.pallas_call(finish, out_shape=[jax.ShapeDtypeStruct((chunk, width), jn...  1.78 us

profile of v4, /device:TPU:0, one launch (start us, length us, event | category | flops | bytes accessed | tf_op | source)
XLA Modules:
  0.0 60.9 jit_solution(16631420157965510734)
XLA Ops:
  0.6 58.5 %shard_map.50 = (f32[96,384]{1,0:T(8,128)}, f32[96,384]{1,0:T(8,128)}, f32[96,384]{1,0:T(8,128)}) custom-call(bf16[3,384,384]{2,1,0:T(8,128)(2,1)} %bitcast.10, s32[1,128]{1,0:T(1,128)} %bitcast.11, f32[1,384]{1,0:T(1,128)} %damp_in.1), custom_call_target="tpu_custom_call" | custom-call | tf_op jit(solution)/shard_map/pallas_call | solution.py:415
  59.1 1.8 %shard_map.51 = (f32[96,384]{1,0:T(8,128)}, f32[96,384]{1,0:T(8,128)}) custom-call(f32[96,384]{1,0:T(8,128)} %get-tuple-element.7.low, f32[96,384]{1,0:T(8,128)} %get-tuple-element.8.pair, f32[96,384]{1,0:T(8,128)} %get-tuple-element.9.carried), custom_call_target="tpu_custom_call" | custom-call | tf_op jit(solution)/shard_map/pallas_call | solution.py:440

commit v5 on v4

--- a/solution.py
+++ b/solution.py
@@ -328,14 +328,14 @@
         3: [(2, late[0])], 4: [(2, late[1])], 5: [(2, late[2])], 7: [(2, late[3])],
         9: [(0, late[0])], 11: [(0, late[1])],
     }
-    sends = {0: late[0], 2: late[1], 3: late[2], 4: late[3]}
+    sends = {1: late[0], 3: late[1], 4: late[2], 5: late[3]}
 
     def between(j):
         for k, b in plan.get(j, ()):
             arrive(k, b)
         if j in sends:
             issue(0, sends[j])
-        if j == 9:
+        if j == 8:
             landed(2, first)
             add_full(1, 2, 1, first)
             full_copy(1).start()

time: 61.1 us -> 60.7 us (level)
  no operation moved by 1% of the time
where the time goes in v5:
time: 60.7 us; the launch traced here: 60.5 us
  Pallas kernels  59.9 us (99%)
  between operations  0.64 us (1%)
    pallas_call x1, Pallas kernels, local(): pl.pallas_call(functools.partial(kernel, owners, groups, rows_per, width,...  58.1 us
    pallas_call x1, Pallas kernels, local(): pl.pallas_call(finish, out_shape=[jax.ShapeDtypeStruct((chunk, width), jn...  1.78 us

profile of v5, /device:TPU:0, one launch (start us, length us, event | category | flops | bytes accessed | tf_op | source)
XLA Modules:
  0.0 60.5 jit_solution(18276015794331822181)
XLA Ops:
  0.6 58.1 %shard_map.50 = (f32[96,384]{1,0:T(8,128)}, f32[96,384]{1,0:T(8,128)}, f32[96,384]{1,0:T(8,128)}) custom-call(bf16[3,384,384]{2,1,0:T(8,128)(2,1)} %bitcast.10, s32[1,128]{1,0:T(1,128)} %bitcast.11, f32[1,384]{1,0:T(1,128)} %damp_in.1), custom_call_target="tpu_custom_call" | custom-call | tf_op jit(solution)/shard_map/pallas_call | solution.py:415
  58.7 1.8 %shard_map.51 = (f32[96,384]{1,0:T(8,128)}, f32[96,384]{1,0:T(8,128)}) custom-call(f32[96,384]{1,0:T(8,128)} %get-tuple-element.7.low, f32[96,384]{1,0:T(8,128)} %get-tuple-element.8.pair, f32[96,384]{1,0:T(8,128)} %get-tuple-element.9.carried), custom_call_target="tpu_custom_call" | custom-call | tf_op jit(solution)/shard_map/pallas_call | solution.py:440
